TPU v7x, 256 devices: a whole 4x4x8 slice. The times are simulated.
256 devices in a mesh: wide: 16 (over y, x), narrow: 16 (over z, core).
Axes of the slice: x: 4, y: 4, z: 8, core: 2. Of those that a mesh axis runs over, the one named last changes fastest.
Arguments:
- vectors: float32 [524288, 128], P(('wide', 'narrow')), may hold values from -24 to 24
- near_blocks: bfloat16 [1024, 3, 512, 512], P(('wide', 'narrow')), may hold values from -0.15625 to 0.15625
- leaf_basis: bfloat16 [524288, 256], P(('wide', 'narrow')), may hold values from -0.125 to 0.125
- transfer: bfloat16 [256, 256, 256], P(('wide', 'narrow')), may hold values from -0.09375 to 0.09375
- leaf_coupling: bfloat16 [256, 6, 256, 256], P(('wide', 'narrow')), may hold values from -0.15625 to 0.15625
- leaf_partners: int32 [256, 6], P(('wide', 'narrow')), may hold values from 0 to 15, as said below
- parent_coupling: bfloat16 [16, 3, 256, 256], P('wide'), may hold values from -0.21875 to 0.21875
- parent_partners: int32 [16, 3], P('wide'), may hold values from 0 to 15, as said below
- shifts: float32 [128], replicated, may hold values from -1 to 1
Outputs:
- filtered: float32 [524288, 128], P(('wide', 'narrow'))
Inputs may be any that keep to these rules, and one draw needn't show every extreme that they name: `leaf_partners`: row l lists 6 different sibling indices, none equal to l mod 16. `parent_partners`: row p lists 3 different parent indices, none equal to p.
All inputs are finite; a program needn't handle non-finite values.
Results may differ from a plain program's by a relative error of at most 0.01.
Values may be sent and summed in bfloat16 or wider, within the bound.
No kernel may reach another device: no remote copies, remote signals or barrier semaphores. Data moves between devices by JAX's collectives and lax.ppermute only.
A program may use at most 64 MiB of HBM per device.

v0:
```python
import functools
import jax
import jax.numpy as jnp
from jax import lax
from jax.sharding import Mesh
from jax.sharding import PartitionSpec as P

BLK = 512
DEGREE = 3
WIDE_NARROW = ("wide_0", "wide_1", "narrow_0", "narrow_1")
NARROW = ("narrow_0", "narrow_1")
WIDE = ("wide_0", "wide_1")


def extended_2(shard, sides, width):
    edges = {}
    for axis, dim in sides:
        size, length = (lax.axis_size(axis), shard.shape[dim])
        up = [(i, (i + 1) % size) for i in range(size - 1)]
        last = lax.slice_in_dim(shard, length - width, length, axis=dim)
        leading = lax.slice_in_dim(shard, 0, width, axis=dim)
        edges[dim] = (
            lax.ppermute(last, axis, up),
            lax.ppermute(leading, axis, [(b, a) for a, b in up]),
        )
    done = []
    for _, dim in sides:
        low, high = edges[dim]
        around = [(width, width) if d in done else (0, 0) for d in range(shard.ndim)]
        shard = jnp.concatenate([jnp.pad(low, around), shard, jnp.pad(high, around)], axis=dim)
        done.append(dim)
    return shard


def whole_of(shard, axes, dim):
    out = shard
    for number in range(len(axes) - 1, -1, -1):
        out = lax.all_gather(out, axes[number], axis=dim, tiled=True)
    return out


def split_up(shard, dim, size):
    lengths = shard.shape
    pieces = shard.reshape(*lengths[:dim], size, lengths[dim] // size, *lengths[dim + 1 :])
    return jnp.moveaxis(pieces, dim, 0)


def summed_on_arrival(shard, axis, dim):
    pieces = split_up(shard, dim, lax.axis_size(axis))
    arrived = lax.all_to_all(pieces, axis, split_axis=0, concat_axis=0, tiled=True)
    return arrived.astype(jnp.float32).sum(axis=0)


def copy_for_each(shard, axis):
    copies = jnp.broadcast_to(shard, (lax.axis_size(axis), *shard.shape))
    return lax.all_to_all(copies, axis, split_axis=0, concat_axis=0, tiled=True)


def joined_along(pieces, dim):
    pieces = jnp.moveaxis(pieces, 0, dim)
    lengths = pieces.shape
    return pieces.reshape(*lengths[:dim], lengths[dim] * lengths[dim + 1], *lengths[dim + 2 :])


def gather_directly(shard, axis, dim):
    pieces = copy_for_each(shard, axis)
    return joined_along(pieces, dim)


def over_axes_2(shard, axes):
    return functools.reduce(lax.psum, axes, shard)


def pick_fold(partners, piece):
    indices = jnp.arange(piece.shape[0], dtype=jnp.int32)
    select = (partners[:, None] == indices[None, :]).astype(jnp.bfloat16)
    return jnp.einsum("jm,mrv->jrv", select, piece, preferred_element_type=jnp.float32)


def shards(
    vectors,
    near_blocks,
    leaf_basis,
    transfer,
    leaf_coupling,
    leaf_partners,
    parent_coupling,
    parent_partners,
    shifts,
):
    local_rows = vectors.shape[0]
    count_blocks = local_rows // BLK
    columns = vectors.shape[1]

    def apply_operator(field):
        vin = field.astype(jnp.bfloat16)
        extended = extended_2(vin, ((WIDE_NARROW, 0),), BLK)
        fields = extended.reshape(count_blocks + 2, BLK, columns)
        near = jnp.einsum(
            "bij,bjv->biv", near_blocks[:, 0], fields[:-2], preferred_element_type=jnp.float32
        )
        near = near + jnp.einsum(
            "bij,bjv->biv", near_blocks[:, 1], fields[1:-1], preferred_element_type=jnp.float32
        )
        near = near + jnp.einsum(
            "bij,bjv->biv", near_blocks[:, 2], fields[2:], preferred_element_type=jnp.float32
        )
        near = near.reshape(local_rows, columns)
        coeff = lax.dot_general(
            leaf_basis, vin, (((0,), (0,)), ((), ())), preferred_element_type=jnp.float32
        )
        coeff_b = coeff.astype(jnp.bfloat16)
        picked = pick_fold(leaf_partners[0], whole_of(coeff_b[None], NARROW, 0))
        leaf_far = jnp.einsum(
            "jrs,jsv->rv",
            leaf_coupling[0],
            picked.astype(jnp.bfloat16),
            preferred_element_type=jnp.float32,
        )
        upward = lax.dot_general(
            transfer[0], coeff_b, (((0,), (0,)), ((), ())), preferred_element_type=jnp.float32
        )
        share = summed_on_arrival(upward.astype(jnp.bfloat16), NARROW, 1)
        top_in = share.astype(jnp.bfloat16)[None]
        gathered = pick_fold(parent_partners[0], gather_directly(top_in, WIDE, 0))
        part_out = jnp.einsum(
            "jrs,jsv->rv",
            parent_coupling[0],
            gathered.astype(jnp.bfloat16),
            preferred_element_type=jnp.float32,
        ).astype(jnp.bfloat16)
        parent_out = lax.all_gather(part_out, NARROW, axis=1, tiled=True)
        downward = jnp.dot(transfer[0], parent_out, preferred_element_type=jnp.float32)
        far_coeff = (leaf_far + downward).astype(jnp.bfloat16)
        return near + jnp.dot(leaf_basis, far_coeff, preferred_element_type=jnp.float32)

    previous = vectors
    current = apply_operator(vectors) - shifts[None, :] * vectors
    for step in range(1, DEGREE):
        following = 2.0 * (apply_operator(current) - shifts[None, :] * current) - previous
        previous, current = (current, following)
    squares = over_axes_2(jnp.sum(current * current, axis=0), WIDE_NARROW)
    total_rows = local_rows * lax.axis_size(WIDE) * lax.axis_size(NARROW)
    meansq = squares / total_rows
    return current / jnp.sqrt(meansq + 1e-06)[None, :]


def solution(mesh):
    finer = Mesh(mesh.devices.reshape(4, 4, 8, 2), ("wide_0", "wide_1", "narrow_0", "narrow_1"))
    placed = (
        P(WIDE_NARROW, None),
        P(WIDE_NARROW, None, None, None),
        P(WIDE_NARROW, None),
        P(WIDE_NARROW, None, None),
        P(WIDE_NARROW, None, None, None),
        P(WIDE_NARROW, None),
        P(WIDE, None, None, None),
        P(WIDE, None),
        P(),
    )
    return jax.shard_map(
        shards, mesh=finer, in_specs=placed, out_specs=P(WIDE_NARROW, None), check_vma=False
    )
```

profile of v0, /device:TPU:1, one launch (start us, length us, event | category | flops | bytes accessed | tf_op | source)
XLA Modules:
  0.0 249.5 jit_solution(17678883639465677823)
XLA Ops:
  6.5 1.4 convert_element_type.102
  8.1 0.5 convolution_convert_fusion.5
  8.6 1.7 fusion.70
  10.3 10.0 %all-to-all-start = ((bf16[16,256,8]{1,2,0:T(8,128)(2,1)}), bf16[16,256,8]{1,2,0:T(8,128)(2,1)S(1)}, u32[]{:S(2)}, u32[]{:S(2)}) async-start(bf16[16,256,8]{1,2,0:T(8,128)(2,1)} %fusion.70), calls=%async_computation | async-start | bytes 131072 | tf_op jit(solution)/shard_map/all_to_all | solution.py:50
  20.3 2.0 all-gather
  22.4 3.5 %collective-permute-start = (bf16[512,128]{1,0:T(8,128)(2,1)S(1)}, bf16[512,128]{1,0:T(8,128)(2,1)S(1)}, u32[]{:S(2)}, u32[]{:S(2)}) collective-permute-start(bf16[512,128]{1,0:T(8,128)(2,1)S(1)} %get-tuple-element.15), channel_id=1, source_target_pairs={{0,1},{1,2},{2,3},{3,4},{4,5},{5,6},{6,7},{7,8},{8,9},{9,10},{10,1... | collective-permute-start | bytes 393224 | tf_op jit(solution)/shard_map/ppermute | solution.py:23
  25.9 1.9 collective-permute-start.1
  27.9 3.4 %fusion.20 = f32[4,512,128]{1,2,0:T(8,128)} fusion(bf16[4,512,128]{2,1,0:T(8,128)(2,1)S(1)} %bitcast.247, bf16[4,3,512,512]{3,2,1,0:T(8,128)(2,1)} %param.10), kind=kOutput, calls=%fused_computation.23 | convolution fusion | flops 268435456 | bytes 3670016 | tf_op jit(solution)/shard_map/bij,bjv->biv/dot_general | solution.py:102
  31.3 1.6 copy.56
  32.9 0.6 broadcast_in_dim.13
  33.5 6.8 %all-to-all-start.1 = ((bf16[16,1,256,8]{2,3,1,0:T(8,128)(2,1)}), bf16[16,1,256,8]{2,3,1,0:T(8,128)(2,1)S(1)}, u32[]{:S(2)}, u32[]{:S(2)}) async-start(bf16[16,1,256,8]{2,3,1,0:T(8,128)(2,1)} %broadcast_in_dim.13), calls=%async_computation.1 | async-start | bytes 131072 | tf_op jit(solution)/shard_map/all_to_all | solution.py:56
  40.4 2.5 %fusion.40 = f32[4,512,128]{1,2,0:T(8,128)S(1)} fusion(bf16[4,512,128]{2,1,0:T(8,128)(2,1)S(1)} %bitcast.251, bf16[4,3,512,512]{3,2,1,0:T(8,128)(2,1)} %param.10), kind=kOutput, calls=%fused_computation.41 | convolution fusion | flops 268435456 | bytes 3670016 | tf_op jit(solution)/shard_map/bij,bjv->biv/dot_general | solution.py:105
  42.9 3.7 %fusion.46 = f32[4,512,128]{1,2,0:T(8,128)} fusion(f32[4,512,128]{1,2,0:T(8,128)S(1)} %fusion.40, f32[4,512,128]{1,2,0:T(8,128)} %fusion.20, bf16[4,512,128]{2,1,0:T(8,128)(2,1)S(1)} %bitcast.254, bf16[4,3,512,512]{3,2,1,0:T(8,128)(2,1)} %param.10), kind=kOutput, calls=%fused_computation.43 | convolution fusion | flops 268959744 | bytes 5767168 | tf_op jit(solution)/shard_map/bij,bjv->biv/dot_general | solution.py:99
  46.7 2.5 %copy.50 = f32[4,512,128]{2,1,0:T(8,128)} copy(f32[4,512,128]{1,2,0:T(8,128)} %fusion.46) | data formatting | bytes 2097152 | tf_op jit(solution)/shard_map/add | solution.py:105
  49.2 2.5 %copy.55 = f32[2048,128]{0,1:T(8,128)} copy(f32[2048,128]{1,0:T(8,128)} %bitcast.249) | data formatting | bytes 2097152 | tf_op jit(solution)/shard_map/reshape | solution.py:108
  52.1 19.2 %all_gather.29 = bf16[256,128]{0,1:T(8,128)(2,1)} all-gather(bf16[256,8]{0,1:T(8,128)(2,1)S(1)} %fusion.78), channel_id=1, replica_groups=mesh['wide_0'=4,'wide_1'=4,'narrow_0'=8,'narrow_1'=2] {'narrow_0','narro..., dimensions={1}, use_global_device_ids=true | all-gather | bytes 69632 | tf_op jit(solution)/shard_map/all_gather | solution.py:132
  71.3 1.9 convolution_convert_fusion.2
  73.2 1.1 convolution_bitcast_fusion.5
  74.3 3.0 %fusion.135 = (bf16[2048,128]{0,1:T(8,128)(2,1)S(1)}, f32[2048,128]{0,1:T(8,128)}) fusion(f32[2048,128]{0,1:T(8,128)S(1)} %copy.56, f32[128]{0:T(128)S(1)} %copy-done.8, f32[2048,128]{0,1:T(8,128)} %copy.55, bf16[2048,256]{1,0:T(8,128)(2,1)S(1)} %copy-done, f32[128,256]{1,0:T(8,128)} %convolution_bitcast_fusion.5, bf16[256,128]{0,1:T(8,128)(2,1)} %all_gather.29, ...), kind=kOutput, calls=%fused_computation.141 | convolution fusion | flops 152109056 | bytes 5046784 | tf_op jit(solution)/shard_map/dot_general | solution.py:135
  77.6 0.6 copy-done.6
  78.2 0.8 fusion.71
  79.0 6.0 %all-to-all-start.2 = ((bf16[16,256,8]{1,2,0:T(8,128)(2,1)}), bf16[16,256,8]{1,2,0:T(8,128)(2,1)}, u32[]{:S(2)}, u32[]{:S(2)}) async-start(bf16[16,256,8]{1,2,0:T(8,128)(2,1)} %fusion.71), calls=%async_computation.2 | async-start | bytes 131072 | tf_op jit(solution)/shard_map/all_to_all | solution.py:50
  85.0 3.4 %all-gather.1 = bf16[512,128]{0,1:T(8,128)(2,1)} all-gather(bf16[256,128]{0,1:T(8,128)(2,1)} %bitcast.257), channel_id=3, replica_groups=mesh['wide_0'=4,'wide_1'=4,'narrow_0'=8,'narrow_1'=2] {'narrow_1'}, dimensions={0}, use_global_device_ids=true | all-gather | bytes 196608 | tf_op jit(solution)/shard_map/all_gather | solution.py:38
  88.3 1.7 copy.80
  90.0 0.7 fusion.133
  90.8 3.5 %collective-permute-start.2 = (bf16[512,128]{0,1:T(8,128)(2,1)}, bf16[512,128]{0,1:T(8,128)(2,1)}, u32[]{:S(2)}, u32[]{:S(2)}) collective-permute-start(bf16[512,128]{0,1:T(8,128)(2,1)} %get-tuple-element.11), channel_id=1, source_target_pairs={{0,1},{1,2},{2,3},{3,4},{4,5},{5,6},{6,7},{7,8},{8,9},{9,10},{10,1... | collective-permute-start | bytes 393224 | tf_op jit(solution)/shard_map/ppermute | solution.py:23
  94.3 1.9 collective-permute-start.3
  96.2 3.4 %fusion.18 = f32[4,128,512]{2,1,0:T(8,128)} fusion(bf16[4,3,512,512]{3,2,1,0:T(8,128)(2,1)} %param.10, bf16[16,4,8,512]{3,2,1,0:T(8,128)(2,1)S(1)} %bitcast.246), kind=kOutput, calls=%fused_computation.21 | convolution fusion | flops 268435456 | bytes 3670016 | tf_op jit(solution)/shard_map/bij,bjv->biv/dot_general | solution.py:102
  99.6 0.9 reduce_sum.46
  100.5 0.6 broadcast_in_dim.15
  101.1 7.0 %all-to-all-start.3 = ((bf16[16,1,256,8]{2,3,1,0:T(8,128)(2,1)}), bf16[16,1,256,8]{2,3,1,0:T(8,128)(2,1)}, u32[]{:S(2)}, u32[]{:S(2)}) async-start(bf16[16,1,256,8]{2,3,1,0:T(8,128)(2,1)} %broadcast_in_dim.15), calls=%async_computation.3 | async-start | bytes 131072 | tf_op jit(solution)/shard_map/all_to_all | solution.py:56
  108.1 1.1 pad_maximum_fusion.3
  109.2 2.5 fusion.12
  111.7 2.7 %fusion.55 = f32[4,16,8,512]{3,2,1,0:T(8,128)S(1)} fusion(f32[4,128,512]{2,1,0:T(8,128)S(1)} %fusion.12, f32[4,128,512]{2,1,0:T(8,128)} %fusion.18, bf16[4,3,512,512]{3,2,1,0:T(8,128)(2,1)} %param.10, bf16[16,4,8,512]{3,2,1,0:T(8,128)(2,1)S(1)} %bitcast.255), kind=kOutput, calls=%fused_computation.46 | convolution fusion | flops 268959744 | bytes 5767168 | tf_op jit(solution)/shard_map/bij,bjv->biv/dot_general | solution.py:99
  114.4 1.0 copy.91
  115.4 1.0 convolution_convert_fusion.10
  116.7 19.6 %all_gather.32 = bf16[256,128]{0,1:T(8,128)(2,1)} all-gather(bf16[256,8]{0,1:T(8,128)(2,1)S(1)} %fusion.77), channel_id=1, replica_groups=mesh['wide_0'=4,'wide_1'=4,'narrow_0'=8,'narrow_1'=2] {'narrow_0','narro..., dimensions={1}, use_global_device_ids=true | all-gather | bytes 69632 | tf_op jit(solution)/shard_map/all_gather | solution.py:132
  136.2 1.9 convolution_convert_fusion.1
  138.1 1.1 convolution_bitcast_fusion.4
  139.2 3.3 %fusion.138 = (bf16[2048,128]{0,1:T(8,128)(2,1)S(1)}, f32[2048,128]{0,1:T(8,128)}) fusion(f32[2048,128]{0,1:T(8,128)S(1)} %copy.56, f32[2048,128]{0,1:T(8,128)} %get-tuple-element.18, f32[128]{0:T(128)S(1)} %copy-done.8, f32[2048,128]{0,1:T(8,128)} %bitcast.248, bf16[2048,256]{1,0:T(8,128)(2,1)S(1)} %copy-done, f32[128,256]{1,0:T(8,128)} %convolution_bitcast_fusion.4, ...), kind=kOutput, calls=%fused_computation.142 | convolution fusion | flops 152633344 | bytes 6095360 | tf_op jit(solution)/shard_map/dot_general | solution.py:135
  142.8 0.8 fusion.72
  143.6 5.9 %all-to-all-start.4 = ((bf16[16,256,8]{1,2,0:T(8,128)(2,1)}), bf16[16,256,8]{1,2,0:T(8,128)(2,1)S(1)}, u32[]{:S(2)}, u32[]{:S(2)}) async-start(bf16[16,256,8]{1,2,0:T(8,128)(2,1)} %fusion.72), calls=%async_computation.4 | async-start | bytes 131072 | tf_op jit(solution)/shard_map/all_to_all | solution.py:50
  149.6 1.9 all-gather.2
  151.5 0.8 copy.81
  152.3 3.5 %collective-permute-start.4 = (bf16[512,128]{0,1:T(8,128)(2,1)S(1)}, bf16[512,128]{0,1:T(8,128)(2,1)S(1)}, u32[]{:S(2)}, u32[]{:S(2)}) collective-permute-start(bf16[512,128]{0,1:T(8,128)(2,1)S(1)} %get-tuple-element.7), channel_id=1, source_target_pairs={{0,1},{1,2},{2,3},{3,4},{4,5},{5,6},{6,7},{7,8},{8,9},{9,10},{10,1... | collective-permute-start | bytes 393224 | tf_op jit(solution)/shard_map/ppermute | solution.py:23
  155.9 1.9 collective-permute-start.5
  157.8 3.4 %fusion.16 = f32[4,128,512]{2,1,0:T(8,128)} fusion(bf16[4,3,512,512]{3,2,1,0:T(8,128)(2,1)} %param.10, bf16[16,4,8,512]{3,2,1,0:T(8,128)(2,1)S(1)} %bitcast.245), kind=kOutput, calls=%fused_computation.19 | convolution fusion | flops 268435456 | bytes 3670016 | tf_op jit(solution)/shard_map/bij,bjv->biv/dot_general | solution.py:102
  161.2 0.6 broadcast_in_dim.17
  161.8 6.5 %all-to-all-start.5 = ((bf16[16,1,256,8]{2,3,1,0:T(8,128)(2,1)}), bf16[16,1,256,8]{2,3,1,0:T(8,128)(2,1)}, u32[]{:S(2)}, u32[]{:S(2)}) async-start(bf16[16,1,256,8]{2,3,1,0:T(8,128)(2,1)} %broadcast_in_dim.17), calls=%async_computation.5 | async-start | bytes 131072 | tf_op jit(solution)/shard_map/all_to_all | solution.py:56
  168.5 2.4 fusion.10
  170.9 2.8 %fusion.64 = f32[4,16,8,512]{3,2,1,0:T(8,128)S(1)} fusion(f32[4,128,512]{2,1,0:T(8,128)S(1)} %fusion.10, f32[4,128,512]{2,1,0:T(8,128)} %fusion.16, bf16[4,3,512,512]{3,2,1,0:T(8,128)(2,1)} %param.10, bf16[16,4,8,512]{3,2,1,0:T(8,128)(2,1)S(1)} %bitcast.256), kind=kOutput, calls=%fused_computation.49 | convolution fusion | flops 268959744 | bytes 5767168 | tf_op jit(solution)/shard_map/bij,bjv->biv/dot_general | solution.py:99
  173.8 1.1 copy.92
  174.9 1.0 convolution_convert_fusion.9
  176.0 1.2 fusion.76
  177.1 19.0 %all_gather.35 = bf16[256,128]{0,1:T(8,128)(2,1)S(1)} all-gather(bf16[256,8]{0,1:T(8,128)(2,1)S(1)} %fusion.76), channel_id=1, replica_groups=mesh['wide_0'=4,'wide_1'=4,'narrow_0'=8,'narrow_1'=2] {'narrow_0','narro..., dimensions={1}, use_global_device_ids=true | all-gather | bytes 69632 | tf_op jit(solution)/shard_map/all_gather | solution.py:132
  196.1 1.9 convolution_convert_fusion
  198.0 0.4 convolution_bitcast_fusion.3
  198.5 3.2 %multiply_reduce_fusion = (f32[128]{0:T(128)S(1)}, f32[2048,128]{0,1:T(8,128)}) fusion(f32[2048,128]{0,1:T(8,128)S(1)} %copy-done.1, f32[2048,128]{0,1:T(8,128)} %get-tuple-element.20, f32[128]{0:T(128)S(1)} %copy-done.8, f32[2048,128]{0,1:T(8,128)} %bitcast.250, bf16[2048,256]{1,0:T(8,128)(2,1)S(1)} %copy-done, ...), kind=kOutput, calls=%fused_computation.86 | convolution fusion | flops 152895360 | bytes 5571584 | tf_op jit(solution)/shard_map/dot_general | solution.py:135
  201.6 7.4 %psum.28 = f32[128]{0:T(128)S(1)} all-reduce(f32[128]{0:T(128)S(1)} %get-tuple-element.21), channel_id=1, replica_groups=mesh['wide_0'=4,'wide_1'=4,'narrow_0'=8,'narrow_1'=2] {'wide_0'}, use_global_device_ids=true, to_apply=%region_4.5 | all-reduce | flops 128 | bytes 1024 | tf_op jit(solution)/shard_map/psum | solution.py:71
  209.1 8.4 %psum.29 = f32[128]{0:T(128)S(1)} all-reduce(f32[128]{0:T(128)S(1)} %psum.28), channel_id=1, replica_groups=mesh['wide_0'=4,'wide_1'=4,'narrow_0'=8,'narrow_1'=2] {'wide_1'}, use_global_device_ids=true, to_apply=%region_5.6 | all-reduce | flops 128 | bytes 1024 | tf_op jit(solution)/shard_map/psum | solution.py:71
  217.4 13.1 %psum.30 = f32[128]{0:T(128)S(1)} all-reduce(f32[128]{0:T(128)S(1)} %psum.29), channel_id=1, replica_groups=mesh['wide_0'=4,'wide_1'=4,'narrow_0'=8,'narrow_1'=2] {'narrow_0'}, use_global_device_ids=true, to_apply=%region_6.7 | all-reduce | flops 128 | bytes 1024 | tf_op jit(solution)/shard_map/psum | solution.py:71
  230.5 9.8 %psum.31 = f32[128]{0:T(128)S(1)} all-reduce(f32[128]{0:T(128)S(1)} %psum.30), channel_id=1, replica_groups=mesh['wide_0'=4,'wide_1'=4,'narrow_0'=8,'narrow_1'=2] {'narrow_1'}, use_global_device_ids=true, to_apply=%region_7.8 | all-reduce | flops 128 | bytes 1024 | tf_op jit(solution)/shard_map/psum | solution.py:71
  240.3 1.4 broadcast_divide_fusion
  241.7 1.3 copy.76
  (52 shorter events, 2.0 us)
Async XLA Ops:
  6.5 1.5 copy-start
  10.3 22.5 %all-to-all-start = ((bf16[16,256,8]{1,2,0:T(8,128)(2,1)}), bf16[16,256,8]{1,2,0:T(8,128)(2,1)S(1)}, u32[]{:S(2)}, u32[]{:S(2)}) async-start(bf16[16,256,8]{1,2,0:T(8,128)(2,1)} %fusion.70), calls=%async_computation | async-start | bytes 131072 | tf_op jit(solution)/shard_map/all_to_all | solution.py:50
  20.3 51.0 %all-gather.7.cloned.1.call-start = ((), (), s32[]{:S(2)}) async-start(), calls=%async_computation.6 | async-start | bytes 1179648 | tf_op jit(solution)/shard_map/all_gather | solution.py:38
  22.4 17.9 %collective-permute-start = (bf16[512,128]{1,0:T(8,128)(2,1)S(1)}, bf16[512,128]{1,0:T(8,128)(2,1)S(1)}, u32[]{:S(2)}, u32[]{:S(2)}) collective-permute-start(bf16[512,128]{1,0:T(8,128)(2,1)S(1)} %get-tuple-element.15), channel_id=1, source_target_pairs={{0,1},{1,2},{2,3},{3,4},{4,5},{5,6},{6,7},{7,8},{8,9},{9,10},{10,1... | collective-permute-start | bytes 393224 | tf_op jit(solution)/shard_map/ppermute | solution.py:23
  25.9 14.3 %collective-permute-start.1 = (bf16[512,128]{1,0:T(8,128)(2,1)S(1)}, bf16[512,128]{1,0:T(8,128)(2,1)S(1)}, u32[]{:S(2)}, u32[]{:S(2)}) collective-permute-start(bf16[512,128]{1,0:T(8,128)(2,1)S(1)} %get-tuple-element.16), channel_id=1, source_target_pairs={{1,0},{2,1},{3,2},{4,3},{5,4},{6,5},{7,6},{8,7},{9,8},{10,9},{11,1... | collective-permute-start | bytes 393224 | tf_op jit(solution)/shard_map/ppermute | solution.py:24
  33.5 18.3 %all-to-all-start.1 = ((bf16[16,1,256,8]{2,3,1,0:T(8,128)(2,1)}), bf16[16,1,256,8]{2,3,1,0:T(8,128)(2,1)S(1)}, u32[]{:S(2)}, u32[]{:S(2)}) async-start(bf16[16,1,256,8]{2,3,1,0:T(8,128)(2,1)} %broadcast_in_dim.13), calls=%async_computation.1 | async-start | bytes 131072 | tf_op jit(solution)/shard_map/all_to_all | solution.py:56
  40.3 11.4 %copy-start.9 = (s32[1,3]{1,0:T(1,128)S(1)}, s32[1,3]{1,0:T(1,128)}, u32[]{:S(2)}) copy-start(s32[1,3]{1,0:T(1,128)} %param.16) | copy-start | bytes 40
  40.3 11.6 %copy-start.4 = (bf16[1,3,256,256]{3,2,1,0:T(8,128)(2,1)S(1)}, bf16[1,3,256,256]{3,2,1,0:T(8,128)(2,1)}, u32[]{:S(2)}) copy-start(bf16[1,3,256,256]{3,2,1,0:T(8,128)(2,1)} %param.15) | copy-start | bytes 1179652
  40.4 30.9 %copy-start.7 = (s32[1,6]{1,0:T(1,128)S(1)}, s32[1,6]{1,0:T(1,128)}, u32[]{:S(2)}) copy-start(s32[1,6]{1,0:T(1,128)} %param.14) | copy-start | bytes 76
  42.9 30.3 %copy-start.2 = (bf16[1,6,256,256]{3,2,1,0:T(8,128)(2,1)S(1)}, bf16[1,6,256,256]{3,2,1,0:T(8,128)(2,1)}, u32[]{:S(2)}) copy-start(bf16[1,6,256,256]{3,2,1,0:T(8,128)(2,1)} %param.13) | copy-start | bytes 2359300
  42.9 31.4 %copy-start.3 = (bf16[1,256,256]{2,1,0:T(8,128)(2,1)S(1)}, bf16[1,256,256]{2,1,0:T(8,128)(2,1)}, u32[]{:S(2)}) copy-start(bf16[1,256,256]{2,1,0:T(8,128)(2,1)} %param.12) | copy-start | bytes 393220
  42.9 31.4 %copy-start.8 = (f32[128]{0:T(128)S(1)}, f32[128]{0:T(128)}, u32[]{:S(2)}) copy-start(f32[128]{0:T(128)} %param.17) | copy-start | bytes 1540
  77.5 0.6 copy-start.6
  79.0 20.6 %all-to-all-start.2 = ((bf16[16,256,8]{1,2,0:T(8,128)(2,1)}), bf16[16,256,8]{1,2,0:T(8,128)(2,1)}, u32[]{:S(2)}, u32[]{:S(2)}) async-start(bf16[16,256,8]{1,2,0:T(8,128)(2,1)} %fusion.71), calls=%async_computation.2 | async-start | bytes 131072 | tf_op jit(solution)/shard_map/all_to_all | solution.py:50
  84.9 51.3 %all-gather.9.cloned.1.call-start = ((), (), s32[]{:S(2)}) async-start(), calls=%async_computation.7 | async-start | bytes 1179648 | tf_op jit(solution)/shard_map/all_gather | solution.py:38
  90.8 17.3 %collective-permute-start.2 = (bf16[512,128]{0,1:T(8,128)(2,1)}, bf16[512,128]{0,1:T(8,128)(2,1)}, u32[]{:S(2)}, u32[]{:S(2)}) collective-permute-start(bf16[512,128]{0,1:T(8,128)(2,1)} %get-tuple-element.11), channel_id=1, source_target_pairs={{0,1},{1,2},{2,3},{3,4},{4,5},{5,6},{6,7},{7,8},{8,9},{9,10},{10,1... | collective-permute-start | bytes 393224 | tf_op jit(solution)/shard_map/ppermute | solution.py:23
  94.3 13.8 %collective-permute-start.3 = (bf16[512,128]{0,1:T(8,128)(2,1)}, bf16[512,128]{0,1:T(8,128)(2,1)}, u32[]{:S(2)}, u32[]{:S(2)}) collective-permute-start(bf16[512,128]{0,1:T(8,128)(2,1)} %get-tuple-element.12), channel_id=1, source_target_pairs={{1,0},{2,1},{3,2},{4,3},{5,4},{6,5},{7,6},{8,7},{9,8},{10,9},{11,1... | collective-permute-start | bytes 393224 | tf_op jit(solution)/shard_map/ppermute | solution.py:24
  101.1 14.3 %all-to-all-start.3 = ((bf16[16,1,256,8]{2,3,1,0:T(8,128)(2,1)}), bf16[16,1,256,8]{2,3,1,0:T(8,128)(2,1)}, u32[]{:S(2)}, u32[]{:S(2)}) async-start(bf16[16,1,256,8]{2,3,1,0:T(8,128)(2,1)} %broadcast_in_dim.15), calls=%async_computation.3 | async-start | bytes 131072 | tf_op jit(solution)/shard_map/all_to_all | solution.py:56
  109.2 7.3 %copy-start.5 = (bf16[1,3,256,256]{3,2,1,0:T(8,128)(2,1)S(1)}, bf16[1,3,256,256]{3,2,1,0:T(8,128)(2,1)}, u32[]{:S(2)}) copy-start(bf16[1,3,256,256]{3,2,1,0:T(8,128)(2,1)} %param.15) | copy-start | bytes 1179652
  143.6 17.6 %all-to-all-start.4 = ((bf16[16,256,8]{1,2,0:T(8,128)(2,1)}), bf16[16,256,8]{1,2,0:T(8,128)(2,1)S(1)}, u32[]{:S(2)}, u32[]{:S(2)}) async-start(bf16[16,256,8]{1,2,0:T(8,128)(2,1)} %fusion.72), calls=%async_computation.4 | async-start | bytes 131072 | tf_op jit(solution)/shard_map/all_to_all | solution.py:50
  149.6 46.6 %all-gather.11.cloned.1.call-start = ((), (), s32[]{:S(2)}) async-start(), calls=%async_computation.8 | async-start | bytes 1179648 | tf_op jit(solution)/shard_map/all_gather | solution.py:38
  152.3 16.1 %collective-permute-start.4 = (bf16[512,128]{0,1:T(8,128)(2,1)S(1)}, bf16[512,128]{0,1:T(8,128)(2,1)S(1)}, u32[]{:S(2)}, u32[]{:S(2)}) collective-permute-start(bf16[512,128]{0,1:T(8,128)(2,1)S(1)} %get-tuple-element.7), channel_id=1, source_target_pairs={{0,1},{1,2},{2,3},{3,4},{4,5},{5,6},{6,7},{7,8},{8,9},{9,10},{10,1... | collective-permute-start | bytes 393224 | tf_op jit(solution)/shard_map/ppermute | solution.py:23
  155.9 12.5 %collective-permute-start.5 = (bf16[512,128]{0,1:T(8,128)(2,1)S(1)}, bf16[512,128]{0,1:T(8,128)(2,1)S(1)}, u32[]{:S(2)}, u32[]{:S(2)}) collective-permute-start(bf16[512,128]{0,1:T(8,128)(2,1)S(1)} %get-tuple-element.8), channel_id=1, source_target_pairs={{1,0},{2,1},{3,2},{4,3},{5,4},{6,5},{7,6},{8,7},{9,8},{10,9},{11,1... | collective-permute-start | bytes 393224 | tf_op jit(solution)/shard_map/ppermute | solution.py:24
  161.8 13.1 %all-to-all-start.5 = ((bf16[16,1,256,8]{2,3,1,0:T(8,128)(2,1)}), bf16[16,1,256,8]{2,3,1,0:T(8,128)(2,1)}, u32[]{:S(2)}, u32[]{:S(2)}) async-start(bf16[16,1,256,8]{2,3,1,0:T(8,128)(2,1)} %broadcast_in_dim.17), calls=%async_computation.5 | async-start | bytes 131072 | tf_op jit(solution)/shard_map/all_to_all | solution.py:56
  170.9 27.5 %copy-start.1 = (f32[2048,128]{0,1:T(8,128)S(1)}, f32[2048,128]{0,1:T(8,128)}, u32[]{:S(2)}) copy-start(f32[2048,128]{0,1:T(8,128)} %get-tuple-element.18) | copy-start | bytes 3145732
Sparse Core Ops, SparseCore 0:
  22.9 35.2 all-gather.6
  90.2 34.5 all-gather.8
  152.4 34.1 all-gather.10
where the time goes:
time: 251 us; the launch traced here: 250 us
  blocking collectives  104 us (41%)
  starting transfers between devices  58.6 us (23%)
  matrix products  52.7 us (21%)
  local copies, waits for them, and re-layouts  15.9 us (6%)
  between operations  13.5 us (5%)
  other arithmetic  4.89 us (2%)
    all_gather x3, blocking collectives, apply_operator(): parent_out = lax.all_gather(part_out, NARROW, axis=1, tiled=True)  57.7 us
    psum x4, blocking collectives, over_axes_2(): return functools.reduce(lax.psum, axes, shard)  38.6 us
    all_to_all x3, starting transfers between devices, summed_on_arrival(): lax.all_to_all(pieces, axis, split_axis=0, concat_axis=0, tiled=True)  21.9 us
    all_to_all x3, starting transfers between devices, copy_for_each(): return lax.all_to_all(copies, axis, split_axis=0, concat_axis=0, tiled=True)  20.3 us
    ppermute x3, starting transfers between devices, extended_2(): lax.ppermute(last, axis, up)  10.6 us
    dot_general x3, matrix products, apply_operator(): jnp.einsum('bij,bjv->biv', near_blocks[:, 1], fields[1:-1], preferred_ele...  10.2 us
    dot_general x3, matrix products, apply_operator(): jnp.dot(leaf_basis, far_coeff, preferred_element_type=jnp.float32)  9.46 us
    dot_general x3, matrix products, apply_operator(): jnp.einsum('bij,bjv->biv', near_blocks[:, 0], fields[:-2], preferred_elem...  9.28 us
  transfers between devices with their start and end apart: 15, of which 1 were waited for; matrix products, arithmetic and copies ran while one was open for 19% of the time, Pallas kernels for 0%

commit v1 on v0

--- a/solution.py
+++ b/solution.py
@@ -129,7 +129,16 @@
             gathered.astype(jnp.bfloat16),
             preferred_element_type=jnp.float32,
         ).astype(jnp.bfloat16)
-        parent_out = lax.all_gather(part_out, NARROW, axis=1, tiled=True)
+        point_yards_up = lambda content: jnp.concatenate(
+            lax.all_to_all(
+                jnp.stack([content] * lax.axis_size(NARROW)),
+                axis_name=NARROW,
+                split_axis=0,
+                concat_axis=0,
+            ),
+            1,
+        )
+        parent_out = point_yards_up(part_out)
         downward = jnp.dot(transfer[0], parent_out, preferred_element_type=jnp.float32)
         far_coeff = (leaf_far + downward).astype(jnp.bfloat16)
         return near + jnp.dot(leaf_basis, far_coeff, preferred_element_type=jnp.float32)

time: 251 us -> 234 us (0.932)
  blocking collectives: 104 us -> 45 us
  starting transfers between devices: 58.6 us -> 82.2 us
  waiting for transfers between devices: 0.21 us -> 15.4 us
  local copies, waits for them, and re-layouts: 15.9 us -> 18.6 us
    all_gather x3 -> x0, blocking collectives: 57.7 us -> none  [apply_operator(): parent_out = lax.all_gather(part_out, NARROW, axis=1, tiled=True)]
    all_to_all x0 -> x3, starting transfers between devices: none -> 28 us  [apply_operator(): lax.all_to_all(jnp.stack([content] * lax.axis_size(NARROW)), axis_name=NA...]
    all_to_all x0 -> x3, waiting for transfers between devices: none -> 15.1 us  [apply_operator(): lax.all_to_all(jnp.stack([content] * lax.axis_size(NARROW)), axis_name=NA...]
    all_to_all x3, starting transfers between devices: 21.9 us -> 17.4 us  [summed_on_arrival(): lax.all_to_all(pieces, axis, split_axis=0, concat_axis=0, tiled=True)]
  transfers between devices with their start and end apart: 15 -> 18, of which waited for: 1 -> 4; matrix products, arithmetic and copies ran while one was open for 19% -> 24% of each run, Pallas kernels for 0% -> 0%
where the time goes in v1:
time: 234 us; the launch traced here: 232 us
  starting transfers between devices  82.2 us (35%)
  matrix products  52.6 us (22%)
  blocking collectives  45 us (19%)
  local copies, waits for them, and re-layouts  18.6 us (8%)
  waiting for transfers between devices  15.4 us (7%)
  between operations  13.5 us (6%)
  other arithmetic  4.9 us (2%)
    psum x4, blocking collectives, over_axes_2(): return functools.reduce(lax.psum, axes, shard)  37.7 us
    all_to_all x3, starting transfers between devices, apply_operator(): lax.all_to_all(jnp.stack([content] * lax.axis_size(NARROW)), axis_name=NA...  28 us
    all_to_all x3, starting transfers between devices, copy_for_each(): return lax.all_to_all(copies, axis, split_axis=0, concat_axis=0, tiled=True)  20.4 us
    all_to_all x3, starting transfers between devices, summed_on_arrival(): lax.all_to_all(pieces, axis, split_axis=0, concat_axis=0, tiled=True)  17.4 us
    all_to_all x3, waiting for transfers between devices, apply_operator(): lax.all_to_all(jnp.stack([content] * lax.axis_size(NARROW)), axis_name=NA...  15.1 us
    ppermute x3, starting transfers between devices, extended_2(): lax.ppermute(last, axis, up)  10.5 us
    dot_general x3, matrix products, apply_operator(): jnp.einsum('bij,bjv->biv', near_blocks[:, 1], fields[1:-1], preferred_ele...  10.1 us
    dot_general x3, matrix products, apply_operator(): jnp.dot(leaf_basis, far_coeff, preferred_element_type=jnp.float32)  9.44 us
  transfers between devices with their start and end apart: 18, of which 4 were waited for; matrix products, arithmetic and copies ran while one was open for 24% of the time, Pallas kernels for 0%

profile of v1, /device:TPU:1, one launch (start us, length us, event | category | flops | bytes accessed | tf_op | source)
XLA Modules:
  0.0 232.2 jit_solution(4796229621980294444)
XLA Ops:
  6.5 1.4 convert_element_type.102
  8.6 1.7 fusion.70
  10.3 10.0 %all-to-all-start = ((bf16[16,256,8]{1,2,0:T(8,128)(2,1)}), bf16[16,256,8]{1,2,0:T(8,128)(2,1)S(1)}, u32[]{:S(2)}, u32[]{:S(2)}) async-start(bf16[16,256,8]{1,2,0:T(8,128)(2,1)} %fusion.70), calls=%async_computation | async-start | bytes 131072 | tf_op jit(solution)/shard_map/all_to_all | solution.py:50
  20.3 2.0 all-gather
  22.4 3.5 %collective-permute-start = (bf16[512,128]{1,0:T(8,128)(2,1)S(1)}, bf16[512,128]{1,0:T(8,128)(2,1)S(1)}, u32[]{:S(2)}, u32[]{:S(2)}) collective-permute-start(bf16[512,128]{1,0:T(8,128)(2,1)S(1)} %get-tuple-element.15), channel_id=1, source_target_pairs={{0,1},{1,2},{2,3},{3,4},{4,5},{5,6},{6,7},{7,8},{8,9},{9,10},{10,1... | collective-permute-start | bytes 393224 | tf_op jit(solution)/shard_map/ppermute | solution.py:23
  25.9 1.9 collective-permute-start.1
  27.9 3.4 %fusion.20 = f32[4,512,128]{1,2,0:T(8,128)} fusion(bf16[4,512,128]{2,1,0:T(8,128)(2,1)S(1)} %bitcast.268, bf16[4,3,512,512]{3,2,1,0:T(8,128)(2,1)} %param.10), kind=kOutput, calls=%fused_computation.23 | convolution fusion | flops 268435456 | bytes 3670016 | tf_op jit(solution)/shard_map/bij,bjv->biv/dot_general | solution.py:102
  31.2 1.6 copy.59
  33.5 6.8 %all-to-all-start.1 = ((bf16[16,1,256,8]{2,3,1,0:T(8,128)(2,1)}), bf16[16,1,256,8]{2,3,1,0:T(8,128)(2,1)S(1)}, u32[]{:S(2)}, u32[]{:S(2)}) async-start(bf16[16,1,256,8]{2,3,1,0:T(8,128)(2,1)} %broadcast_in_dim.13), calls=%async_computation.1 | async-start | bytes 131072 | tf_op jit(solution)/shard_map/all_to_all | solution.py:56
  40.4 2.5 %fusion.40 = f32[4,512,128]{1,2,0:T(8,128)S(1)} fusion(bf16[4,512,128]{2,1,0:T(8,128)(2,1)S(1)} %bitcast.272, bf16[4,3,512,512]{3,2,1,0:T(8,128)(2,1)} %param.10), kind=kOutput, calls=%fused_computation.41 | convolution fusion | flops 268435456 | bytes 3670016 | tf_op jit(solution)/shard_map/bij,bjv->biv/dot_general | solution.py:105
  42.9 3.8 %fusion.46 = f32[4,512,128]{1,2,0:T(8,128)} fusion(f32[4,512,128]{1,2,0:T(8,128)S(1)} %fusion.40, f32[4,512,128]{1,2,0:T(8,128)} %fusion.20, bf16[4,512,128]{2,1,0:T(8,128)(2,1)S(1)} %bitcast.275, bf16[4,3,512,512]{3,2,1,0:T(8,128)(2,1)} %param.10), kind=kOutput, calls=%fused_computation.43 | convolution fusion | flops 268959744 | bytes 5767168 | tf_op jit(solution)/shard_map/bij,bjv->biv/dot_general | solution.py:99
  46.7 2.5 %copy.53 = f32[4,512,128]{2,1,0:T(8,128)} copy(f32[4,512,128]{1,2,0:T(8,128)} %fusion.46) | data formatting | bytes 2097152 | tf_op jit(solution)/shard_map/add | solution.py:105
  49.2 2.5 %copy.58 = f32[2048,128]{0,1:T(8,128)} copy(f32[2048,128]{1,0:T(8,128)} %bitcast.270) | data formatting | bytes 2097152 | tf_op jit(solution)/shard_map/reshape | solution.py:108
  52.1 0.7 stack.6
  52.8 8.8 %all-to-all-start.2 = ((bf16[16,256,8]{1,2,0:T(8,128)(2,1)}), bf16[16,256,8]{1,2,0:T(8,128)(2,1)}, u32[]{:S(2)}, u32[]{:S(2)}) async-start(bf16[16,256,8]{1,2,0:T(8,128)(2,1)} %stack.6), calls=%async_computation.2 | async-start | bytes 131072 | tf_op jit(solution)/shard_map/all_to_all | solution.py:133
  61.7 1.9 convolution_convert_fusion.2
  63.6 1.1 convolution_bitcast_fusion.5
  64.6 4.9 %all-to-all-done.2 = bf16[16,256,8]{1,2,0:T(8,128)(2,1)} async-done(((bf16[16,256,8]{1,2,0:T(8,128)(2,1)}), bf16[16,256,8]{1,2,0:T(8,128)(2,1)}, u32[]{:S(2)}, u32[]{:S(2)}) %all-to-all-start.2) | async-done | bytes 65568 | tf_op jit(solution)/shard_map/all_to_all | solution.py:133
  69.5 3.0 %fusion.141 = (bf16[2048,128]{0,1:T(8,128)(2,1)S(1)}, f32[2048,128]{0,1:T(8,128)}) fusion(f32[2048,128]{0,1:T(8,128)S(1)} %copy.59, f32[128]{0:T(128)S(1)} %copy-done.9, f32[2048,128]{0,1:T(8,128)} %copy.58, bf16[2048,256]{1,0:T(8,128)(2,1)S(1)} %copy-done, f32[128,256]{1,0:T(8,128)} %convolution_bitcast_fusion.5, bf16[1,256,256]{2,1,0:T(8,128)(2,1)S(1)} %copy-done.3, ...), kind=kOutput, calls=%fused_computation.144 | convolution fusion | flops 152109056 | bytes 5046784 | tf_op jit(solution)/shard_map/dot_general | solution.py:144
  73.4 0.8 fusion.71
  74.2 4.0 %all-to-all-start.3 = ((bf16[16,256,8]{1,2,0:T(8,128)(2,1)}), bf16[16,256,8]{1,2,0:T(8,128)(2,1)}, u32[]{:S(2)}, u32[]{:S(2)}) async-start(bf16[16,256,8]{1,2,0:T(8,128)(2,1)} %fusion.71), calls=%async_computation.3 | async-start | bytes 131072 | tf_op jit(solution)/shard_map/all_to_all | solution.py:50
  78.3 3.4 %all-gather.1 = bf16[512,128]{0,1:T(8,128)(2,1)} all-gather(bf16[256,128]{0,1:T(8,128)(2,1)} %bitcast.278), channel_id=3, replica_groups=mesh['wide_0'=4,'wide_1'=4,'narrow_0'=8,'narrow_1'=2] {'narrow_1'}, dimensions={0}, use_global_device_ids=true | all-gather | bytes 196608 | tf_op jit(solution)/shard_map/all_gather | solution.py:38
  81.7 1.6 copy.83
  83.4 0.7 fusion.139
  84.1 3.4 %collective-permute-start.2 = (bf16[512,128]{0,1:T(8,128)(2,1)}, bf16[512,128]{0,1:T(8,128)(2,1)}, u32[]{:S(2)}, u32[]{:S(2)}) collective-permute-start(bf16[512,128]{0,1:T(8,128)(2,1)} %get-tuple-element.11), channel_id=1, source_target_pairs={{0,1},{1,2},{2,3},{3,4},{4,5},{5,6},{6,7},{7,8},{8,9},{9,10},{10,1... | collective-permute-start | bytes 393224 | tf_op jit(solution)/shard_map/ppermute | solution.py:23
  87.5 1.9 collective-permute-start.3
  89.4 3.4 %fusion.18 = f32[4,128,512]{2,1,0:T(8,128)} fusion(bf16[4,3,512,512]{3,2,1,0:T(8,128)(2,1)} %param.10, bf16[16,4,8,512]{3,2,1,0:T(8,128)(2,1)S(1)} %bitcast.267), kind=kOutput, calls=%fused_computation.21 | convolution fusion | flops 268435456 | bytes 3670016 | tf_op jit(solution)/shard_map/bij,bjv->biv/dot_general | solution.py:102
  92.8 0.9 reduce_sum.46
  94.3 7.0 %all-to-all-start.4 = ((bf16[16,1,256,8]{2,3,1,0:T(8,128)(2,1)}), bf16[16,1,256,8]{2,3,1,0:T(8,128)(2,1)}, u32[]{:S(2)}, u32[]{:S(2)}) async-start(bf16[16,1,256,8]{2,3,1,0:T(8,128)(2,1)} %broadcast_in_dim.15), calls=%async_computation.4 | async-start | bytes 131072 | tf_op jit(solution)/shard_map/all_to_all | solution.py:56
  101.3 1.1 pad_maximum_fusion.3
  102.4 2.5 %fusion.12 = f32[4,128,512]{2,1,0:T(8,128)S(1)} fusion(bf16[4,3,512,512]{3,2,1,0:T(8,128)(2,1)} %param.10, bf16[16,4,8,512]{3,2,1,0:T(8,128)(2,1)S(1)} %bitcast.273), kind=kOutput, calls=%fused_computation.15 | convolution fusion | flops 268435456 | bytes 3670016 | tf_op jit(solution)/shard_map/bij,bjv->biv/dot_general | solution.py:105
  104.9 2.7 %fusion.55 = f32[4,16,8,512]{3,2,1,0:T(8,128)S(1)} fusion(f32[4,128,512]{2,1,0:T(8,128)S(1)} %fusion.12, f32[4,128,512]{2,1,0:T(8,128)} %fusion.18, bf16[4,3,512,512]{3,2,1,0:T(8,128)(2,1)} %param.10, bf16[16,4,8,512]{3,2,1,0:T(8,128)(2,1)S(1)} %bitcast.276), kind=kOutput, calls=%fused_computation.46 | convolution fusion | flops 268959744 | bytes 5767168 | tf_op jit(solution)/shard_map/bij,bjv->biv/dot_general | solution.py:99
  107.6 1.0 copy.94
  108.6 1.0 convolution_convert_fusion.10
  109.9 0.7 stack.7
  110.6 9.2 %all-to-all-start.5 = ((bf16[16,256,8]{1,2,0:T(8,128)(2,1)}), bf16[16,256,8]{1,2,0:T(8,128)(2,1)S(1)}, u32[]{:S(2)}, u32[]{:S(2)}) async-start(bf16[16,256,8]{1,2,0:T(8,128)(2,1)} %stack.7), calls=%async_computation.5 | async-start | bytes 131072 | tf_op jit(solution)/shard_map/all_to_all | solution.py:133
  119.8 1.9 convolution_convert_fusion.1
  121.7 1.1 convolution_bitcast_fusion.4
  122.8 4.8 %all-to-all-done.5 = bf16[16,256,8]{1,2,0:T(8,128)(2,1)S(1)} async-done(((bf16[16,256,8]{1,2,0:T(8,128)(2,1)}), bf16[16,256,8]{1,2,0:T(8,128)(2,1)S(1)}, u32[]{:S(2)}, u32[]{:S(2)}) %all-to-all-start.5) | async-done | bytes 65568 | tf_op jit(solution)/shard_map/all_to_all | solution.py:133
  128.2 3.3 %fusion.146 = (bf16[2048,128]{0,1:T(8,128)(2,1)S(1)}, f32[2048,128]{0,1:T(8,128)}) fusion(f32[2048,128]{0,1:T(8,128)S(1)} %copy.59, f32[2048,128]{0,1:T(8,128)} %get-tuple-element.18, f32[128]{0:T(128)S(1)} %copy-done.9, f32[2048,128]{0,1:T(8,128)} %bitcast.269, bf16[2048,256]{1,0:T(8,128)(2,1)S(1)} %copy-done, f32[128,256]{1,0:T(8,128)} %convolution_bitcast_fusion.4, ...), kind=kOutput, calls=%fused_computation.145 | convolution fusion | flops 152633344 | bytes 6095360 | tf_op jit(solution)/shard_map/dot_general | solution.py:144
  131.8 0.8 fusion.72
  132.6 3.4 %all-to-all-start.6 = ((bf16[16,256,8]{1,2,0:T(8,128)(2,1)}), bf16[16,256,8]{1,2,0:T(8,128)(2,1)S(1)}, u32[]{:S(2)}, u32[]{:S(2)}) async-start(bf16[16,256,8]{1,2,0:T(8,128)(2,1)} %fusion.72), calls=%async_computation.6 | async-start | bytes 131072 | tf_op jit(solution)/shard_map/all_to_all | solution.py:50
  136.0 1.9 all-gather.2
  137.9 0.7 copy.84
  138.7 3.5 %collective-permute-start.4 = (bf16[512,128]{0,1:T(8,128)(2,1)S(1)}, bf16[512,128]{0,1:T(8,128)(2,1)S(1)}, u32[]{:S(2)}, u32[]{:S(2)}) collective-permute-start(bf16[512,128]{0,1:T(8,128)(2,1)S(1)} %get-tuple-element.7), channel_id=1, source_target_pairs={{0,1},{1,2},{2,3},{3,4},{4,5},{5,6},{6,7},{7,8},{8,9},{9,10},{10,1... | collective-permute-start | bytes 393224 | tf_op jit(solution)/shard_map/ppermute | solution.py:23
  142.3 1.9 collective-permute-start.5
  144.2 3.4 %fusion.16 = f32[4,128,512]{2,1,0:T(8,128)} fusion(bf16[4,3,512,512]{3,2,1,0:T(8,128)(2,1)} %param.10, bf16[16,4,8,512]{3,2,1,0:T(8,128)(2,1)S(1)} %bitcast.266), kind=kOutput, calls=%fused_computation.19 | convolution fusion | flops 268435456 | bytes 3670016 | tf_op jit(solution)/shard_map/bij,bjv->biv/dot_general | solution.py:102
  148.3 6.6 %all-to-all-start.7 = ((bf16[16,1,256,8]{2,3,1,0:T(8,128)(2,1)}), bf16[16,1,256,8]{2,3,1,0:T(8,128)(2,1)}, u32[]{:S(2)}, u32[]{:S(2)}) async-start(bf16[16,1,256,8]{2,3,1,0:T(8,128)(2,1)} %broadcast_in_dim.17), calls=%async_computation.7 | async-start | bytes 131072 | tf_op jit(solution)/shard_map/all_to_all | solution.py:56
  155.0 2.4 %fusion.10 = f32[4,128,512]{2,1,0:T(8,128)S(1)} fusion(bf16[4,3,512,512]{3,2,1,0:T(8,128)(2,1)} %param.10, bf16[16,4,8,512]{3,2,1,0:T(8,128)(2,1)S(1)} %bitcast.274), kind=kOutput, calls=%fused_computation.13 | convolution fusion | flops 268435456 | bytes 3670016 | tf_op jit(solution)/shard_map/bij,bjv->biv/dot_general | solution.py:105
  157.5 2.8 %fusion.64 = f32[4,16,8,512]{3,2,1,0:T(8,128)S(1)} fusion(f32[4,128,512]{2,1,0:T(8,128)S(1)} %fusion.10, f32[4,128,512]{2,1,0:T(8,128)} %fusion.16, bf16[4,3,512,512]{3,2,1,0:T(8,128)(2,1)} %param.10, bf16[16,4,8,512]{3,2,1,0:T(8,128)(2,1)S(1)} %bitcast.277), kind=kOutput, calls=%fused_computation.49 | convolution fusion | flops 268959744 | bytes 5767168 | tf_op jit(solution)/shard_map/bij,bjv->biv/dot_general | solution.py:99
  160.3 1.1 copy.95
  161.5 1.0 convolution_convert_fusion.9
  162.5 1.2 fusion.76
  163.7 0.7 stack.8
  164.4 10.0 %all-to-all-start.8 = ((bf16[16,256,8]{1,2,0:T(8,128)(2,1)}), bf16[16,256,8]{1,2,0:T(8,128)(2,1)S(1)}, u32[]{:S(2)}, u32[]{:S(2)}) async-start(bf16[16,256,8]{1,2,0:T(8,128)(2,1)} %stack.8), calls=%async_computation.8 | async-start | bytes 131072 | tf_op jit(solution)/shard_map/all_to_all | solution.py:133
  174.4 1.9 convolution_convert_fusion
  176.7 5.4 %all-to-all-done.8 = bf16[16,256,8]{1,2,0:T(8,128)(2,1)S(1)} async-done(((bf16[16,256,8]{1,2,0:T(8,128)(2,1)}), bf16[16,256,8]{1,2,0:T(8,128)(2,1)S(1)}, u32[]{:S(2)}, u32[]{:S(2)}) %all-to-all-start.8) | async-done | bytes 65568 | tf_op jit(solution)/shard_map/all_to_all | solution.py:133
  182.1 3.2 %multiply_reduce_fusion = (f32[128]{0:T(128)S(1)}, f32[2048,128]{0,1:T(8,128)}) fusion(f32[2048,128]{0,1:T(8,128)S(1)} %copy-done.1, f32[2048,128]{0,1:T(8,128)} %get-tuple-element.20, f32[128]{0:T(128)S(1)} %copy-done.9, f32[2048,128]{0,1:T(8,128)} %bitcast.271, bf16[2048,256]{1,0:T(8,128)(2,1)S(1)} %copy-done, ...), kind=kOutput, calls=%fused_computation.86 | convolution fusion | flops 152895360 | bytes 5571584 | tf_op jit(solution)/shard_map/dot_general | solution.py:144
  185.3 7.3 %psum.28 = f32[128]{0:T(128)S(1)} all-reduce(f32[128]{0:T(128)S(1)} %get-tuple-element.21), channel_id=1, replica_groups=mesh['wide_0'=4,'wide_1'=4,'narrow_0'=8,'narrow_1'=2] {'wide_0'}, use_global_device_ids=true, to_apply=%region_4.5 | all-reduce | flops 128 | bytes 1024 | tf_op jit(solution)/shard_map/psum | solution.py:71
  192.6 8.5 %psum.29 = f32[128]{0:T(128)S(1)} all-reduce(f32[128]{0:T(128)S(1)} %psum.28), channel_id=1, replica_groups=mesh['wide_0'=4,'wide_1'=4,'narrow_0'=8,'narrow_1'=2] {'wide_1'}, use_global_device_ids=true, to_apply=%region_5.6 | all-reduce | flops 128 | bytes 1024 | tf_op jit(solution)/shard_map/psum | solution.py:71
  201.2 10.8 %psum.30 = f32[128]{0:T(128)S(1)} all-reduce(f32[128]{0:T(128)S(1)} %psum.29), channel_id=1, replica_groups=mesh['wide_0'=4,'wide_1'=4,'narrow_0'=8,'narrow_1'=2] {'narrow_0'}, use_global_device_ids=true, to_apply=%region_6.7 | all-reduce | flops 128 | bytes 1024 | tf_op jit(solution)/shard_map/psum | solution.py:71
  212.0 10.9 %psum.31 = f32[128]{0:T(128)S(1)} all-reduce(f32[128]{0:T(128)S(1)} %psum.30), channel_id=1, replica_groups=mesh['wide_0'=4,'wide_1'=4,'narrow_0'=8,'narrow_1'=2] {'narrow_1'}, use_global_device_ids=true, to_apply=%region_7.8 | all-reduce | flops 128 | bytes 1024 | tf_op jit(solution)/shard_map/psum | solution.py:71
  223.0 1.4 broadcast_divide_fusion
  224.4 1.3 copy.79
  (60 shorter events, 6.0 us)
Async XLA Ops:
  6.5 1.5 copy-start
  10.3 22.5 %all-to-all-start = ((bf16[16,256,8]{1,2,0:T(8,128)(2,1)}), bf16[16,256,8]{1,2,0:T(8,128)(2,1)S(1)}, u32[]{:S(2)}, u32[]{:S(2)}) async-start(bf16[16,256,8]{1,2,0:T(8,128)(2,1)} %fusion.70), calls=%async_computation | async-start | bytes 131072 | tf_op jit(solution)/shard_map/all_to_all | solution.py:50
  20.3 41.4 %all-gather.7.cloned.1.call-start = ((), (), s32[]{:S(2)}) async-start(), calls=%async_computation.9 | async-start | bytes 1179648 | tf_op jit(solution)/shard_map/all_gather | solution.py:38
  22.4 17.9 %collective-permute-start = (bf16[512,128]{1,0:T(8,128)(2,1)S(1)}, bf16[512,128]{1,0:T(8,128)(2,1)S(1)}, u32[]{:S(2)}, u32[]{:S(2)}) collective-permute-start(bf16[512,128]{1,0:T(8,128)(2,1)S(1)} %get-tuple-element.15), channel_id=1, source_target_pairs={{0,1},{1,2},{2,3},{3,4},{4,5},{5,6},{6,7},{7,8},{8,9},{9,10},{10,1... | collective-permute-start | bytes 393224 | tf_op jit(solution)/shard_map/ppermute | solution.py:23
  25.9 14.3 %collective-permute-start.1 = (bf16[512,128]{1,0:T(8,128)(2,1)S(1)}, bf16[512,128]{1,0:T(8,128)(2,1)S(1)}, u32[]{:S(2)}, u32[]{:S(2)}) collective-permute-start(bf16[512,128]{1,0:T(8,128)(2,1)S(1)} %get-tuple-element.16), channel_id=1, source_target_pairs={{1,0},{2,1},{3,2},{4,3},{5,4},{6,5},{7,6},{8,7},{9,8},{10,9},{11,1... | collective-permute-start | bytes 393224 | tf_op jit(solution)/shard_map/ppermute | solution.py:24
  33.5 18.2 %all-to-all-start.1 = ((bf16[16,1,256,8]{2,3,1,0:T(8,128)(2,1)}), bf16[16,1,256,8]{2,3,1,0:T(8,128)(2,1)S(1)}, u32[]{:S(2)}, u32[]{:S(2)}) async-start(bf16[16,1,256,8]{2,3,1,0:T(8,128)(2,1)} %broadcast_in_dim.13), calls=%async_computation.1 | async-start | bytes 131072 | tf_op jit(solution)/shard_map/all_to_all | solution.py:56
  40.3 11.4 %copy-start.10 = (s32[1,3]{1,0:T(1,128)S(1)}, s32[1,3]{1,0:T(1,128)}, u32[]{:S(2)}) copy-start(s32[1,3]{1,0:T(1,128)} %param.16) | copy-start | bytes 40
  40.3 11.6 %copy-start.4 = (bf16[1,3,256,256]{3,2,1,0:T(8,128)(2,1)S(1)}, bf16[1,3,256,256]{3,2,1,0:T(8,128)(2,1)}, u32[]{:S(2)}) copy-start(bf16[1,3,256,256]{3,2,1,0:T(8,128)(2,1)} %param.15) | copy-start | bytes 1179652
  40.4 21.3 %copy-start.8 = (s32[1,6]{1,0:T(1,128)S(1)}, s32[1,6]{1,0:T(1,128)}, u32[]{:S(2)}) copy-start(s32[1,6]{1,0:T(1,128)} %param.14) | copy-start | bytes 76
  42.9 20.7 %copy-start.2 = (bf16[1,6,256,256]{3,2,1,0:T(8,128)(2,1)S(1)}, bf16[1,6,256,256]{3,2,1,0:T(8,128)(2,1)}, u32[]{:S(2)}) copy-start(bf16[1,6,256,256]{3,2,1,0:T(8,128)(2,1)} %param.13) | copy-start | bytes 2359300
  42.9 26.6 %copy-start.3 = (bf16[1,256,256]{2,1,0:T(8,128)(2,1)S(1)}, bf16[1,256,256]{2,1,0:T(8,128)(2,1)}, u32[]{:S(2)}) copy-start(bf16[1,256,256]{2,1,0:T(8,128)(2,1)} %param.12) | copy-start | bytes 393220
  42.9 26.6 %copy-start.9 = (f32[128]{0:T(128)S(1)}, f32[128]{0:T(128)}, u32[]{:S(2)}) copy-start(f32[128]{0:T(128)} %param.17) | copy-start | bytes 1540
  52.8 16.7 %all-to-all-start.2 = ((bf16[16,256,8]{1,2,0:T(8,128)(2,1)}), bf16[16,256,8]{1,2,0:T(8,128)(2,1)}, u32[]{:S(2)}, u32[]{:S(2)}) async-start(bf16[16,256,8]{1,2,0:T(8,128)(2,1)} %stack.6), calls=%async_computation.2 | async-start | bytes 131072 | tf_op jit(solution)/shard_map/all_to_all | solution.py:133
  72.8 0.6 copy-start.6
  74.2 18.6 %all-to-all-start.3 = ((bf16[16,256,8]{1,2,0:T(8,128)(2,1)}), bf16[16,256,8]{1,2,0:T(8,128)(2,1)}, u32[]{:S(2)}, u32[]{:S(2)}) async-start(bf16[16,256,8]{1,2,0:T(8,128)(2,1)} %fusion.71), calls=%async_computation.3 | async-start | bytes 131072 | tf_op jit(solution)/shard_map/all_to_all | solution.py:50
  78.2 41.6 %all-gather.9.cloned.1.call-start = ((), (), s32[]{:S(2)}) async-start(), calls=%async_computation.10 | async-start | bytes 1179648 | tf_op jit(solution)/shard_map/all_gather | solution.py:38
  84.1 17.2 %collective-permute-start.2 = (bf16[512,128]{0,1:T(8,128)(2,1)}, bf16[512,128]{0,1:T(8,128)(2,1)}, u32[]{:S(2)}, u32[]{:S(2)}) collective-permute-start(bf16[512,128]{0,1:T(8,128)(2,1)} %get-tuple-element.11), channel_id=1, source_target_pairs={{0,1},{1,2},{2,3},{3,4},{4,5},{5,6},{6,7},{7,8},{8,9},{9,10},{10,1... | collective-permute-start | bytes 393224 | tf_op jit(solution)/shard_map/ppermute | solution.py:23
  87.5 13.8 %collective-permute-start.3 = (bf16[512,128]{0,1:T(8,128)(2,1)}, bf16[512,128]{0,1:T(8,128)(2,1)}, u32[]{:S(2)}, u32[]{:S(2)}) collective-permute-start(bf16[512,128]{0,1:T(8,128)(2,1)} %get-tuple-element.12), channel_id=1, source_target_pairs={{1,0},{2,1},{3,2},{4,3},{5,4},{6,5},{7,6},{8,7},{9,8},{10,9},{11,1... | collective-permute-start | bytes 393224 | tf_op jit(solution)/shard_map/ppermute | solution.py:24
  94.3 14.3 %all-to-all-start.4 = ((bf16[16,1,256,8]{2,3,1,0:T(8,128)(2,1)}), bf16[16,1,256,8]{2,3,1,0:T(8,128)(2,1)}, u32[]{:S(2)}, u32[]{:S(2)}) async-start(bf16[16,1,256,8]{2,3,1,0:T(8,128)(2,1)} %broadcast_in_dim.15), calls=%async_computation.4 | async-start | bytes 131072 | tf_op jit(solution)/shard_map/all_to_all | solution.py:56
  102.4 7.3 %copy-start.5 = (bf16[1,3,256,256]{3,2,1,0:T(8,128)(2,1)S(1)}, bf16[1,3,256,256]{3,2,1,0:T(8,128)(2,1)}, u32[]{:S(2)}) copy-start(bf16[1,3,256,256]{3,2,1,0:T(8,128)(2,1)} %param.15) | copy-start | bytes 1179652
  110.6 17.0 %all-to-all-start.5 = ((bf16[16,256,8]{1,2,0:T(8,128)(2,1)}), bf16[16,256,8]{1,2,0:T(8,128)(2,1)S(1)}, u32[]{:S(2)}, u32[]{:S(2)}) async-start(bf16[16,256,8]{1,2,0:T(8,128)(2,1)} %stack.7), calls=%async_computation.5 | async-start | bytes 131072 | tf_op jit(solution)/shard_map/all_to_all | solution.py:133
  127.6 0.6 copy-start.7
  132.6 15.0 %all-to-all-start.6 = ((bf16[16,256,8]{1,2,0:T(8,128)(2,1)}), bf16[16,256,8]{1,2,0:T(8,128)(2,1)S(1)}, u32[]{:S(2)}, u32[]{:S(2)}) async-start(bf16[16,256,8]{1,2,0:T(8,128)(2,1)} %fusion.72), calls=%async_computation.6 | async-start | bytes 131072 | tf_op jit(solution)/shard_map/all_to_all | solution.py:50
  136.0 38.3 %all-gather.11.cloned.1.call-start = ((), (), s32[]{:S(2)}) async-start(), calls=%async_computation.11 | async-start | bytes 1179648 | tf_op jit(solution)/shard_map/all_gather | solution.py:38
  138.7 16.2 %collective-permute-start.4 = (bf16[512,128]{0,1:T(8,128)(2,1)S(1)}, bf16[512,128]{0,1:T(8,128)(2,1)S(1)}, u32[]{:S(2)}, u32[]{:S(2)}) collective-permute-start(bf16[512,128]{0,1:T(8,128)(2,1)S(1)} %get-tuple-element.7), channel_id=1, source_target_pairs={{0,1},{1,2},{2,3},{3,4},{4,5},{5,6},{6,7},{7,8},{8,9},{9,10},{10,1... | collective-permute-start | bytes 393224 | tf_op jit(solution)/shard_map/ppermute | solution.py:23
  142.3 12.6 %collective-permute-start.5 = (bf16[512,128]{0,1:T(8,128)(2,1)S(1)}, bf16[512,128]{0,1:T(8,128)(2,1)S(1)}, u32[]{:S(2)}, u32[]{:S(2)}) collective-permute-start(bf16[512,128]{0,1:T(8,128)(2,1)S(1)} %get-tuple-element.8), channel_id=1, source_target_pairs={{1,0},{2,1},{3,2},{4,3},{5,4},{6,5},{7,6},{8,7},{9,8},{10,9},{11,1... | collective-permute-start | bytes 393224 | tf_op jit(solution)/shard_map/ppermute | solution.py:24
  148.3 13.2 %all-to-all-start.7 = ((bf16[16,1,256,8]{2,3,1,0:T(8,128)(2,1)}), bf16[16,1,256,8]{2,3,1,0:T(8,128)(2,1)}, u32[]{:S(2)}, u32[]{:S(2)}) async-start(bf16[16,1,256,8]{2,3,1,0:T(8,128)(2,1)} %broadcast_in_dim.17), calls=%async_computation.7 | async-start | bytes 131072 | tf_op jit(solution)/shard_map/all_to_all | solution.py:56
  157.5 24.7 %copy-start.1 = (f32[2048,128]{0,1:T(8,128)S(1)}, f32[2048,128]{0,1:T(8,128)}, u32[]{:S(2)}) copy-start(f32[2048,128]{0,1:T(8,128)} %get-tuple-element.18) | copy-start | bytes 3145732
  164.4 17.7 %all-to-all-start.8 = ((bf16[16,256,8]{1,2,0:T(8,128)(2,1)}), bf16[16,256,8]{1,2,0:T(8,128)(2,1)S(1)}, u32[]{:S(2)}, u32[]{:S(2)}) async-start(bf16[16,256,8]{1,2,0:T(8,128)(2,1)} %stack.8), calls=%async_computation.8 | async-start | bytes 131072 | tf_op jit(solution)/shard_map/all_to_all | solution.py:133
Sparse Core Ops, SparseCore 0:
  22.8 35.2 all-gather.6
  83.5 34.5 all-gather.8
  138.8 34.2 all-gather.10
